TPU v7x, 32 devices: a whole 2x2x4 slice. The times are simulated.
32 devices in a mesh: gx: 16 (over z, y, core), gy: 2 (over x).
Axes of the slice: x: 2, y: 2, z: 4, core: 2. Of those that a mesh axis runs over, the one named last changes fastest.
Arguments:
- old_block: float32 [12288, 24576], P('gx', 'gy'), may hold values from -6 to 6
- vectors: bfloat16 [256, 2, 12288], P(None, 'gy', 'gx'), may hold values from -4 to 4
- prior: bfloat16 [32768, 3072], P('gx', 'gy'), may hold values from -2 to 2
- pair_columns: float32 [32768, 128], P(('gx', 'gy')), may hold values from -6 to 6
- pivots: int32 [128], replicated, may hold values from 0 to 32767
Outputs:
- new_block: float32 [12288, 24576], P('gx', 'gy')
- residual_columns: float32 [32768, 128], P(('gx', 'gy'))
Inputs may be any that keep to these rules, and one draw needn't show every extreme that they name: `pivots`: pivot AO-pair row indices, repeats possible.
All inputs are finite; a program needn't handle non-finite values.
Results may differ from a plain program's by a relative error of at most 0.0055.
Values may be sent and summed in bfloat16 or wider, within the bound.
A program may use at most 192 MiB of HBM per device.

v0:
```python
import jax
import jax.numpy as jnp
from jax import lax
from jax.sharding import PartitionSpec as P


def from_root(value, axis, root):
    mine = lax.axis_index(axis) == root
    return lax.psum(jnp.where(mine, value, jnp.zeros_like(value)), axis)


def local(old_block, vectors, prior, pair_columns, pivots):
    local_vectors = vectors.reshape(vectors.shape[0], vectors.shape[2])
    slab_part = from_root(local_vectors, "gy", 0)
    gained = jnp.dot(
        slab_part.T,
        lax.all_gather(local_vectors, "gx", axis=1, tiled=True),
        preferred_element_type=jnp.float32,
    )
    new_block = old_block + gained
    rows_local = prior.shape[0]
    offset = lax.axis_index("gx") * rows_local
    local_index = pivots - offset
    inside = jnp.logical_and(local_index >= 0, local_index < rows_local)
    chosen = jnp.take(prior, jnp.clip(local_index, 0, rows_local - 1), axis=0).astype(jnp.float32)
    chosen = chosen * inside[:, None].astype(jnp.float32)
    pivot_block = lax.psum(chosen.astype(jnp.bfloat16), "gx")
    groups = lax.axis_size("gy")
    width = prior.shape[1]
    regrouped = lax.all_to_all(prior, "gy", split_axis=0, concat_axis=1, tiled=True)
    full_pivots = lax.all_gather(pivot_block, "gy", axis=1, tiled=True)
    parts = jnp.einsum(
        "rgc,kgc->grk",
        regrouped.reshape(regrouped.shape[0], groups, width),
        full_pivots.reshape(full_pivots.shape[0], groups, width),
        preferred_element_type=jnp.float32,
    )
    rounded = lax.optimization_barrier(parts.astype(jnp.bfloat16))
    intersection = jnp.sum(rounded.astype(jnp.float32), axis=0)
    return (new_block, pair_columns - intersection)


def solution(mesh):
    placed = (P("gx", "gy"), P(None, "gy", "gx"), P("gx", "gy"), P(("gx", "gy"), None), P())
    return jax.shard_map(
        local,
        mesh=mesh,
        in_specs=placed,
        out_specs=(P("gx", "gy"), P(("gx", "gy"), None)),
        check_vma=False,
    )
```

profile of v0, /device:TPU:0, one launch (start us, length us, event | category | flops | bytes accessed | tf_op | source)
XLA Modules:
  0.0 236.3 jit_solution(9439408910341760958)
XLA Ops:
  7.2 0.0 all-reduce.5.cloned.1.call-start
  7.2 0.7 compare_and_fusion
  7.9 4.8 %gather_fusion = bf16[128,1536]{1,0:T(8,128)(2,1)S(1)} fusion(bf16[2048,1536]{1,0:T(8,128)(2,1)} %param.7, s32[1024]{0:T(1024)S(1)} %pad_clamp_fusion), kind=kCustom, calls=%fused_computation | custom fusion | bytes 786944 | tf_op jit(solution)/shard_map/jit(_take)/gather | solution.py:25
  12.7 0.9 multiply_convert_fusion
  13.7 0.0 all-reduce.5.cloned.1.call-update
  13.7 0.0 all-reduce.3.cloned.1.call-start
  13.8 1.8 select_bitcast_fusion
  15.6 0.0 all-reduce.3.cloned.1.call-update
  15.6 0.0 all-gather.3.cloned.1.call-start
  15.6 0.7 all-gather.3.cloned.1.call-update
  16.3 0.0 copy-start
  16.3 6.5 %all-to-all-start = ((bf16[2,1024,1536]{2,1,0:T(8,128)(2,1)}), bf16[2,1024,1536]{2,1,0:T(8,128)(2,1)}, u32[]{:S(2)}, u32[]{:S(2)}) async-start(bf16[2,1024,1536]{2,1,0:T(8,128)(2,1)} %bitcast.18), calls=%async_computation | async-start | bytes 12582912 | tf_op jit(solution)/shard_map/all_to_all | solution.py:30
  22.8 0.2 copy.11
  23.0 84.9 %all-reduce.5.cloned.1.call-done = bf16[128,1536]{1,0:T(8,128)(2,1)} async-done(((bf16[128,1536]{1,0:T(8,128)(2,1)}), bf16[128,1536]{1,0:T(8,128)(2,1)}) %all-reduce.5.cloned.1.call-update) | async-done | bytes 393232 | tf_op jit(solution)/shard_map/psum | solution.py:27
  107.9 14.1 %all_gather.7 = bf16[128,3072]{1,0:T(8,128)(2,1)S(1)} all-gather(bf16[128,1536]{1,0:T(8,128)(2,1)} %all-reduce.5.cloned.1.call-done), channel_id=1, replica_groups=mesh['gx'=16,'gy'=2] {'gy'}, dimensions={1}, use_global_device_ids=true | all-gather | bytes 1179648 | tf_op jit(solution)/shard_map/all_gather | solution.py:31
  122.1 0.4 copy.9
  122.4 0.0 all-to-all-done
  122.4 5.0 %fusion.6 = bf16[2,1024,128]{1,2,0:T(8,128)(2,1)S(1)} fusion(bf16[128,2,1536]{0,2,1:T(8,128)(2,1)S(1)} %bitcast.19, bf16[2,1024,1536]{2,1,0:T(8,128)(2,1)} %all-to-all-done), kind=kOutput, calls=%fused_computation.6 | convolution fusion | flops 805568512 | bytes 7602176 | tf_op jit(solution)/shard_map/rgc,kgc->grk/dot_general | solution.py:32
  127.5 0.1 convert_reduce_fusion
  127.6 0.1 sub.11
  127.6 1.0 copy.12
  128.6 7.6 %all-reduce.3.cloned.1.call-done = bf16[256,768]{1,0:T(8,128)(2,1)} async-done(((bf16[256,768]{1,0:T(8,128)(2,1)}), bf16[256,768]{1,0:T(8,128)(2,1)}) %all-reduce.3.cloned.1.call-update) | async-done | bytes 393232 | tf_op jit(solution)/shard_map/psum | solution.py:9
  136.2 63.9 %all-gather.3.cloned.1.call-done = bf16[256,1,12288]{2,0,1:T(8,128)(2,1)} async-done(((bf16[256,1,768]{2,0,1:T(8,128)(2,1)}), bf16[256,1,12288]{2,0,1:T(8,128)(2,1)}) %all-gather.3.cloned.1.call-update) | async-done | bytes 6291472 | tf_op jit(solution)/shard_map/all_gather | solution.py:17
  200.1 29.6 %convolution_add_fusion = f32[768,12288]{1,0:T(8,128)} fusion(f32[768,12288]{1,0:T(8,128)} %param.5, bf16[256,768]{1,0:T(8,128)(2,1)} %all-reduce.3.cloned.1.call-done, bf16[256,1,12288]{2,0,1:T(8,128)(2,1)} %all-gather.3.cloned.1.call-done), kind=kOutput, calls=%fused_computation.1 | convolution fusion | flops 4841275392 | bytes 82182144 | tf_op jit(solution)/shard_map/dot_general | solution.py:15
  (2 shorter events, 0.0 us)
Async XLA Ops:
  7.2 100.7 %all-reduce.5.cloned.1.call-start = ((), (), s32[]{:S(2)}) async-start(), calls=%async_computation.2 | async-start | bytes 786432 | tf_op jit(solution)/shard_map/psum | solution.py:27
  13.7 122.5 %all-reduce.3.cloned.1.call-start = ((), (), s32[]{:S(2)}) async-start(), calls=%async_computation.1 | async-start | bytes 786432 | tf_op jit(solution)/shard_map/psum | solution.py:9
  15.6 184.5 %all-gather.3.cloned.1.call-start = ((), (), s32[]{:S(2)}) async-start(), calls=%async_computation.3 | async-start | bytes 6684672 | tf_op jit(solution)/shard_map/all_gather | solution.py:17
  16.3 6.5 %copy-start = (f32[1024,128]{1,0:T(8,128)S(1)}, f32[1024,128]{1,0:T(8,128)}, u32[]{:S(2)}) copy-start(f32[1024,128]{1,0:T(8,128)} %param.8) | copy-start | bytes 1572868
  16.3 106.1 %all-to-all-start = ((bf16[2,1024,1536]{2,1,0:T(8,128)(2,1)}), bf16[2,1024,1536]{2,1,0:T(8,128)(2,1)}, u32[]{:S(2)}, u32[]{:S(2)}) async-start(bf16[2,1024,1536]{2,1,0:T(8,128)(2,1)} %bitcast.18), calls=%async_computation | async-start | bytes 12582912 | tf_op jit(solution)/shard_map/all_to_all | solution.py:30
Sparse Core Ops, SparseCore 0:
  13.8 94.0 all-reduce.4
  110.8 25.4 all-reduce.2
  138.5 61.5 all-gather.2
where the time goes:
time: 237 us; the launch traced here: 236 us
  waiting for transfers between devices  157 us (66%)
  matrix products  34.7 us (15%)
  blocking collectives  14.1 us (6%)
  between operations  13.8 us (6%)
  starting transfers between devices  6.59 us (3%)
  local copies, waits for them, and re-layouts  6.42 us (3%)
  other arithmetic  3.57 us (2%)
    psum x1, waiting for transfers between devices, local(): pivot_block = lax.psum(chosen.astype(jnp.bfloat16), 'gx')  84.9 us
    all_gather x1, waiting for transfers between devices, local(): lax.all_gather(local_vectors, 'gx', axis=1, tiled=True)  63.9 us
    dot_general x1, matrix products, local(): jnp.dot(slab_part.T, lax.all_gather(local_vectors, 'gx', axis=1, tiled=Tr...  29.6 us
    all_gather x1, blocking collectives, local(): full_pivots = lax.all_gather(pivot_block, 'gy', axis=1, tiled=True)  14.1 us
    psum x1, waiting for transfers between devices, from_root(): return lax.psum(jnp.where(mine, value, jnp.zeros_like(value)), axis)  7.58 us
    all_to_all x1, starting transfers between devices, local(): lax.all_to_all(prior, 'gy', split_axis=0, concat_axis=1, tiled=True)  6.47 us
    dot_general x1, matrix products, local(): jnp.einsum('rgc,kgc->grk', regrouped.reshape(regrouped.shape[0], groups,...  5.02 us
    gather x1, local copies, waits for them, and re-layouts, local(): jnp.take(prior, jnp.clip(local_index, 0, rows_local - 1), axis=0)  4.85 us
  transfers between devices with their start and end apart: 4, of which 3 were waited for; matrix products, arithmetic and copies ran while one was open for 4% of the time, Pallas kernels for 0%

commit v1 on v0

v1 whole, which is shorter than its diff:
```python
import functools

import jax
import jax.numpy as jnp
from jax import lax
from jax.experimental import pallas as pl
from jax.experimental.pallas import tpu as pltpu
from jax.sharding import PartitionSpec as P

F32 = jnp.float32
BF16 = jnp.bfloat16
MESH = pl.DeviceIdType.MESH


def from_root(value, axis, root):
    mine = lax.axis_index(axis) == root
    return lax.psum(jnp.where(mine, value, jnp.zeros_like(value)), axis)


def plain(old_block, vectors, prior, pair_columns, pivots):
    local_vectors = vectors.reshape(vectors.shape[0], vectors.shape[2])
    slab_part = from_root(local_vectors, "gy", 0)
    gained = jnp.dot(slab_part.T, lax.all_gather(local_vectors, "gx", axis=1, tiled=True), preferred_element_type=F32)
    new_block = old_block + gained
    rows_local = prior.shape[0]
    local_index = pivots - lax.axis_index("gx") * rows_local
    inside = jnp.logical_and(local_index >= 0, local_index < rows_local)
    chosen = jnp.take(prior, jnp.clip(local_index, 0, rows_local - 1), axis=0)
    chosen = jnp.where(inside[:, None], chosen, jnp.zeros_like(chosen))
    pivot_block = lax.psum(chosen, "gx")
    part = jnp.dot(prior, pivot_block.T, preferred_element_type=F32).astype(BF16)
    parts = lax.all_to_all(part.reshape(lax.axis_size("gy"), -1, part.shape[1]), "gy", split_axis=0, concat_axis=0)
    rounded = lax.optimization_barrier(parts)
    return new_block, pair_columns - jnp.sum(rounded.astype(F32), axis=0)


def kernel(n, m, vec_ref, prior_ref, old_ref, pair_ref, piv_ref, acc, resid, held, slab, slab_t, prior, wide, chosen,
           half_in, half, rs_in, pick, parts, parts_in, vec_sem, prior_sem, old_sem, own_sem,
           v_send, v_recv, s_send, s_recv, d_send, d_recv, rs_send, rs_recv, ag_send, ag_recv, p_send, p_recv):
    depth, width = vec_ref.shape
    line = n // 4
    chips = n // 2
    gx, gy = lax.axis_index("gx"), lax.axis_index("gy")
    pos, y, core = gx // 4, lax.rem(gx // 2, 2), lax.rem(gx, 2)
    chip = gx // 2
    rows_of = prior.shape[0] // m
    each = chosen.shape[2]

    def at(p, yy, c):
        return (p * 2 + yy) * 2 + c

    prior_in = pltpu.make_async_copy(prior_ref, prior, prior_sem)
    vec_in = pltpu.make_async_copy(vec_ref, held.at[gx], vec_sem)
    vec_in.start()
    prior_in.start()

    def old_copy(block):
        columns = pl.ds(pl.multiple_of(block * width, 128), width)
        return pltpu.make_async_copy(old_ref.at[:, columns], acc.at[:, columns], old_sem.at[block])

    barrier = pltpu.get_barrier_semaphore()
    for step in range(1, n):
        pl.semaphore_signal(barrier, inc=1, device_id=(lax.rem(gx + step, n), gy), device_id_type=MESH)
    for step in range(1, m):
        pl.semaphore_signal(barrier, inc=1, device_id=(gx, lax.rem(gy + step, m)), device_id_type=MESH)
    pl.semaphore_wait(barrier, n - 1 + m - 1)

    sent = []

    def send(copy, when=None):
        def begin():
            copy.start()
        if when is None:
            begin()
        else:
            pl.when(when)(begin)
        sent.append((copy, when))

    def block_copy(src, way, target):
        return pltpu.make_async_remote_copy(held.at[src], held.at[src], v_send.at[src, way], v_recv.at[src], device_id=(target, gy), device_id_type=MESH)

    def arrived(src):
        block_copy(src, 0, gx).wait_recv()

    vec_in.wait()
    send(block_copy(gx, 0, at(pos + 1, y, core)), pos + 1 < line)
    send(block_copy(gx, 1, at(pos - 1, y, core)), pos > 0)
    send(block_copy(gx, 2, at(pos, 1 - y, core)))
    for step in range(1, m):
        copy = pltpu.make_async_remote_copy(held.at[gx], slab, s_send.at[step - 1], s_recv, device_id=(gx, lax.rem(gy + step, m)), device_id_type=MESH)
        send(copy, gy == 0)
    send(block_copy(gx, 3, at(pos, y, 1 - core)))

    prior_in.wait()
    for step in range(n):
        old_copy(step).start()
    local_index = piv_ref[...] - chip_rows(gx, prior)
    onehot = (lax.broadcasted_iota(jnp.int32, (piv_ref.shape[0], prior.shape[0]), 1) == local_index).astype(F32).astype(BF16)
    tile = 256

    def pick_tile(i, _):
        columns = pl.ds(pl.multiple_of(i * tile, tile), tile)
        wide[:, columns] = jnp.dot(onehot, prior[:, columns], preferred_element_type=F32)
        return 0
    lax.fori_loop(0, prior.shape[1] // tile, pick_tile, 0)
    for i in range(n):
        chosen[i // chips, i % chips] = wide[i * each:(i + 1) * each, :].astype(BF16)
    first = pltpu.make_async_remote_copy(chosen.at[1 - core], half_in, d_send.at[0], d_recv.at[0], device_id=(at(pos, y, 1 - core), gy), device_id_type=MESH)

    @pl.when(gy == 0)
    def _():
        own = pltpu.make_async_copy(vec_ref, slab, own_sem)
        own.start()
        own.wait()
    send(first)

    first.wait_recv()
    for i in range(chips):
        half[i] = (chosen[core, i].astype(F32) + half_in[i].astype(F32)).astype(BF16)

    def line_round(step):
        for way, src_pos, ok in ((0, pos - step, pos - step >= 0), (1, pos + step, pos + step < line)):
            src = at(src_pos, y, core)

            @pl.when(ok)
            def _():
                arrived(src)
            onward = pos + 1 if way == 0 else pos - 1
            more = jnp.logical_and(ok, onward < line) if way == 0 else jnp.logical_and(ok, onward >= 0)
            send(block_copy(src, 2, at(pos, 1 - y, core)), ok)
            send(block_copy(src, way, at(onward, y, core)), more)
            send(block_copy(src, 3, at(pos, y, 1 - core)), ok)

    def over_y(src_pos, ok):
        src = at(src_pos, 1 - y, core)

        def go():
            arrived(src)
            block_copy(src, 3, at(pos, y, 1 - core)).start()
        if ok is None:
            go()
        else:
            pl.when(ok)(go)
        sent.append((block_copy(src, 3, at(pos, y, 1 - core)), ok))

    def update(block):
        old_copy(block).wait()
        columns = pl.ds(pl.multiple_of(block * width, 128), width)

        def rows_step(i, _):
            rows = pl.ds(pl.multiple_of(i * tile, tile), tile)
            acc[rows, columns] += jnp.dot(slab_t[rows, :], held[block], preferred_element_type=F32)
            return 0
        lax.fori_loop(0, acc.shape[0] // tile, rows_step, 0)

    def updates(src_pos, yy, c, ok, wait):
        def go():
            src = at(src_pos, yy, c)
            if wait:
                arrived(src)
            update(src)
        if ok is None:
            go()
        else:
            pl.when(ok)(go)

    for step in range(1, chips):
        other = lax.rem(chip + step, chips)
        send(pltpu.make_async_remote_copy(half.at[other], rs_in.at[step - 1], rs_send.at[step - 1], rs_recv.at[step - 1], device_id=(other * 2 + core, gy), device_id_type=MESH))

    line_round(1)

    total = half[chip].astype(F32)
    for step in range(1, chips):
        pltpu.make_async_remote_copy(half.at[chip], rs_in.at[step - 1], rs_send.at[step - 1], rs_recv.at[step - 1], device_id=(gx, gy), device_id_type=MESH).wait_recv()
        total = total + rs_in[step - 1].astype(F32)
    pick[core, chip] = total.astype(BF16)

    @pl.when(gy != 0)
    def _():
        pltpu.make_async_remote_copy(held.at[gx], slab, s_send.at[0], s_recv, device_id=(gx, gy), device_id_type=MESH).wait_recv()
    slab_t[...] = slab[...].T

    for step in range(1, chips):
        other = lax.rem(chip + step, chips)
        send(pltpu.make_async_remote_copy(pick.at[core, chip], pick.at[core, chip], ag_send.at[step - 1], ag_recv.at[step - 1], device_id=(other * 2 + core, gy), device_id_type=MESH))

    over_y(pos, None)
    updates(pos, y, core, None, False)
    updates(pos, y, 1 - core, None, True)
    for src_pos, ok in ((pos - 1, pos >= 1), (pos + 1, pos + 1 < line)):
        updates(src_pos, y, core, ok, False)

    line_round(2)
    for step in range(1, chips):
        other = lax.rem(chip + chips - step, chips)
        pltpu.make_async_remote_copy(pick.at[core, other], pick.at[core, other], ag_send.at[step - 1], ag_recv.at[step - 1], device_id=(gx, gy), device_id_type=MESH).wait_recv()
    last = pltpu.make_async_remote_copy(pick.at[core], pick.at[core], d_send.at[1], d_recv.at[1], device_id=(at(pos, y, 1 - core), gy), device_id_type=MESH)
    send(last)
    for src_pos, ok in ((pos - 1, pos >= 1), (pos + 1, pos + 1 < line)):
        over_y(src_pos, ok)
        updates(src_pos, y, 1 - core, ok, True)
    updates(pos, 1 - y, core, None, False)
    updates(pos, 1 - y, 1 - core, None, True)

    pltpu.make_async_remote_copy(pick.at[1 - core], pick.at[1 - core], d_send.at[1], d_recv.at[1], device_id=(gx, gy), device_id_type=MESH).wait_recv()
    for i in range(n):
        wide[i * each:(i + 1) * each, :] = pick[i // chips, i % chips].astype(F32)
    picked = wide[...].astype(BF16)

    def part_rows(g):
        def go(i, _):
            rows = pl.ds(pl.multiple_of(i * tile, tile), tile)
            source = pl.ds(pl.multiple_of(g * rows_of + i * tile, tile), tile)
            parts[g, rows, :] = lax.dot_general(prior[source, :], picked, (((1,), (1,)), ((), ())), preferred_element_type=F32).astype(BF16)
            return 0
        lax.fori_loop(0, rows_of // tile, go, 0)

    for g in range(m):
        part_rows(g)

    for step in range(2, line):
        if step > 2:
            line_round(step)
        if step == 2:
            for k in range(1, m):
                to = lax.rem(gy + k, m)
                send(pltpu.make_async_remote_copy(parts.at[to], parts_in.at[k - 1], p_send.at[k - 1], p_recv.at[k - 1], device_id=(gx, to), device_id_type=MESH))
        for src_pos, ok in ((pos - step, pos >= step), (pos + step, pos + step < line)):
            updates(src_pos, y, core, ok, False)
            updates(src_pos, y, 1 - core, ok, True)
        before = step - 1
        for src_pos, ok in ((pos - before, pos >= before), (pos + before, pos + before < line)):
            updates(src_pos, 1 - y, core, ok, False)
            updates(src_pos, 1 - y, 1 - core, ok, True)
        for src_pos, ok in ((pos - step, pos >= step), (pos + step, pos + step < line)):
            over_y(src_pos, ok)
    step = line - 1
    for src_pos, ok in ((pos - step, pos >= step), (pos + step, pos + step < line)):
        updates(src_pos, 1 - y, core, ok, False)
        updates(src_pos, 1 - y, 1 - core, ok, True)

    total = parts[gy].astype(F32)
    for k in range(1, m):
        pltpu.make_async_remote_copy(parts.at[gy], parts_in.at[k - 1], p_send.at[k - 1], p_recv.at[k - 1], device_id=(gx, gy), device_id_type=MESH).wait_recv()
        total = total + parts_in[k - 1].astype(F32)
    resid[...] = pair_ref[...] - total

    for copy, when in sent:
        if when is None:
            copy.wait_send()
        else:
            pl.when(when)(copy.wait_send)


def chip_rows(gx, prior):
    return gx * prior.shape[0]


def fused(n, m, old_block, vectors, prior, pair_columns, pivots):
    depth, width = vectors.shape[0], vectors.shape[2]
    rows, columns = old_block.shape
    keys, prior_width = pivots.shape[0], prior.shape[1]
    each, chips = keys // n, n // 2
    rows_of = prior.shape[0] // m
    dma = pltpu.SemaphoreType.DMA
    anywhere = pl.BlockSpec(memory_space=pl.ANY)
    vmem = pl.BlockSpec(memory_space=pltpu.VMEM)
    return pl.pallas_call(
        functools.partial(kernel, n, m),
        out_shape=(pltpu.VMEM((rows, columns), F32), jax.ShapeDtypeStruct(pair_columns.shape, F32)),
        in_specs=[anywhere, anywhere, anywhere, vmem, vmem],
        out_specs=(vmem, vmem),
        scratch_shapes=[
            pltpu.VMEM((n, depth, width), BF16),
            pltpu.VMEM((depth, width), BF16),
            pltpu.VMEM((width, depth), BF16),
            pltpu.VMEM(prior.shape, BF16),
            pltpu.VMEM((keys, prior_width), F32),
            pltpu.VMEM((2, chips, each, prior_width), BF16),
            pltpu.VMEM((chips, each, prior_width), BF16),
            pltpu.VMEM((chips, each, prior_width), BF16),
            pltpu.VMEM((chips - 1, each, prior_width), BF16),
            pltpu.VMEM((2, chips, each, prior_width), BF16),
            pltpu.VMEM((m, rows_of, keys), BF16),
            pltpu.VMEM((m - 1, rows_of, keys), BF16),
            dma, dma, dma((n,)), dma,
            dma((n, 4)), dma((n,)), dma((m - 1,)), dma, dma((2,)), dma((2,)),
            dma((chips - 1,)), dma((chips - 1,)), dma((chips - 1,)), dma((chips - 1,)), dma((m - 1,)), dma((m - 1,)),
        ],
        compiler_params=pltpu.CompilerParams(collective_id=0, has_side_effects=True, vmem_limit_bytes=VMEM_LIMIT),
    )(vectors.reshape(depth, width), prior, old_block, pair_columns, pivots.reshape(keys, 1))


VMEM_LIMIT = 26 * 1024 * 1024


def solution(mesh):
    n, m = mesh.shape["gx"], mesh.shape["gy"]

    def local(old_block, vectors, prior, pair_columns, pivots):
        width = vectors.shape[2]
        whole_tiles = width % 256 == 0 and prior.shape[1] % 256 == 0 and prior.shape[0] // m % 256 == 0
        if n % 4 == 0 and n >= 12 and m >= 2 and pivots.shape[0] % (8 * n) == 0 and whole_tiles:
            return fused(n, m, old_block, vectors, prior, pair_columns, pivots)
        return plain(old_block, vectors, prior, pair_columns, pivots)

    placed = (P("gx", "gy"), P(None, "gy", "gx"), P("gx", "gy"), P(("gx", "gy"), None), P())
    return jax.shard_map(
        local,
        mesh=mesh,
        in_specs=placed,
        out_specs=(P("gx", "gy"), P(("gx", "gy"), None)),
        check_vma=False,
    )
```

time: 237 us -> 78.1 us (0.33)
  waiting for transfers between devices: 157 us -> 0 us
  Pallas kernels: 0 us -> 61.6 us
  matrix products: 34.7 us -> 0 us
  blocking collectives: 14.1 us -> 0 us
  between operations: 13.8 us -> 0.65 us
  local copies, waits for them, and re-layouts: 6.42 us -> 15.3 us
  starting transfers between devices: 6.59 us -> 0 us
  other arithmetic: 3.57 us -> 0 us
    psum x2 -> x0, waiting for transfers between devices: 92.5 us -> none  [the longest x1 84.9 us: local(): pivot_block = lax.psum(chosen.astype(jnp.bfloat16), 'gx')]
    all_gather x1 -> x0, waiting for transfers between devices: 63.9 us -> none  [local(): lax.all_gather(local_vectors, 'gx', axis=1, tiled=True)]
    pallas_call x0 -> x1, Pallas kernels: none -> 61.6 us  [fused(): pl.pallas_call(functools.partial(kernel, n, m), out_shape=(pltpu.VMEM((ro...]
    dot_general x2 -> x0, matrix products: 34.7 us -> none  [the longest x1 29.6 us: local(): jnp.dot(slab_part.T, lax.all_gather(local_vectors, 'gx', axis=1, tiled=Tr...]
    all_gather x1 -> x0, blocking collectives: 14.1 us -> none  [local(): full_pivots = lax.all_gather(pivot_block, 'gy', axis=1, tiled=True)]
    unnamed x4, local copies, waits for them, and re-layouts: 1.2 us -> 13.9 us
    all_to_all x1 -> x0, starting transfers between devices: 6.47 us -> none  [local(): lax.all_to_all(prior, 'gy', split_axis=0, concat_axis=1, tiled=True)]
    gather x1 -> x0, local copies, waits for them, and re-layouts: 4.85 us -> none  [local(): jnp.take(prior, jnp.clip(local_index, 0, rows_local - 1), axis=0)]
  transfers between devices with their start and end apart: 4 -> 0, of which waited for: 3 -> 0; matrix products, arithmetic and copies ran while one was open for 4% -> 0% of each run, Pallas kernels for 0% -> 0%
where the time goes in v1:
time: 78.1 us; the launch traced here: 77.5 us
  Pallas kernels  61.6 us (79%)
  local copies, waits for them, and re-layouts  15.3 us (20%)
    pallas_call x1, Pallas kernels, fused(): pl.pallas_call(functools.partial(kernel, n, m), out_shape=(pltpu.VMEM((ro...  61.6 us
    unnamed x4, local copies, waits for them, and re-layouts  13.9 us

profile of v1, /device:TPU:0, one launch (start us, length us, event | category | flops | bytes accessed | tf_op | source)
XLA Modules:
  0.0 77.5 jit_solution(14351218233276280811)
XLA Ops:
  0.6 1.4 %copy.7.piv_ref = s32[128,1]{1,0:T(8,128)} copy(s32[128,1]{0,1:T(1,128)} %bitcast.3) | data formatting | bytes 1024 | tf_op jit(solution)/shard_map/reshape | solution.py:292
  2.0 61.6 %shard_map.68 = (f32[768,12288]{1,0:T(8,128)S(1)}, f32[1024,128]{1,0:T(8,128)}) custom-call(bf16[256,768]{1,0:T(8,128)(2,1)} %bitcast.2, bf16[2048,1536]{1,0:T(8,128)(2,1)} %prior_ref.1, f32[768,12288]{1,0:T(8,128)} %old_ref.1, f32[1024,128]{1,0:T(8,128)} %pair_ref.1, s32[128,1]{1,0:T(8,128)} %copy.7.piv_ref), custom_call_target="tpu_custom_call" | custom-call | tf_op jit(solution)/shard_map/pallas_call | solution.py:269
  63.7 0.0 copy-start
  63.7 13.1 %copy.10 = f32[768,12288]{1,0:T(8,128)} copy(f32[768,12288]{1,0:T(8,128)S(1)} %get-tuple-element.2) | data formatting | bytes 75497472
  76.7 0.0 copy-done
  76.7 0.8 %copy.11 = f32[1024,128]{1,0:T(8,128)} copy(f32[1024,128]{1,0:T(8,128)S(1)} %copy-done) | data formatting | bytes 1048576
Async XLA Ops:
  63.7 13.1 %copy-start = (f32[1024,128]{1,0:T(8,128)S(1)}, f32[1024,128]{1,0:T(8,128)}, u32[]{:S(2)}) copy-start(f32[1024,128]{1,0:T(8,128)} %get-tuple-element.7) | copy-start | bytes 1572868

commit v2 on v1

v2 whole, which is shorter than its diff:
```python
import functools

import jax
import jax.numpy as jnp
from jax import lax
from jax.experimental import pallas as pl
from jax.experimental.pallas import tpu as pltpu
from jax.sharding import PartitionSpec as P

F32 = jnp.float32
BF16 = jnp.bfloat16
MESH = pl.DeviceIdType.MESH


def from_root(value, axis, root):
    mine = lax.axis_index(axis) == root
    return lax.psum(jnp.where(mine, value, jnp.zeros_like(value)), axis)


def plain(old_block, vectors, prior, pair_columns, pivots):
    local_vectors = vectors.reshape(vectors.shape[0], vectors.shape[2])
    slab_part = from_root(local_vectors, "gy", 0)
    gained = jnp.dot(slab_part.T, lax.all_gather(local_vectors, "gx", axis=1, tiled=True), preferred_element_type=F32)
    new_block = old_block + gained
    rows_local = prior.shape[0]
    local_index = pivots - lax.axis_index("gx") * rows_local
    inside = jnp.logical_and(local_index >= 0, local_index < rows_local)
    chosen = jnp.take(prior, jnp.clip(local_index, 0, rows_local - 1), axis=0)
    chosen = jnp.where(inside[:, None], chosen, jnp.zeros_like(chosen))
    pivot_block = lax.psum(chosen, "gx")
    part = jnp.dot(prior, pivot_block.T, preferred_element_type=F32).astype(BF16)
    parts = lax.all_to_all(part.reshape(lax.axis_size("gy"), -1, part.shape[1]), "gy", split_axis=0, concat_axis=0)
    rounded = lax.optimization_barrier(parts)
    return new_block, pair_columns - jnp.sum(rounded.astype(F32), axis=0)


def kernel(n, m, pieces, vec_ref, prior_ref, old_ref, pair_ref, piv_ref, acc, resid, held, slab_t, slab, prior, wide, chosen,
           half_in, half, rs_in, pick, parts, parts_in, vec_sem, prior_sem, old_sem, own_sem,
           v_send, v_recv, s_send, s_recv, d_send, d_recv, rs_send, rs_recv, ag_send, ag_recv, p_send, p_recv):
    depth, width = vec_ref.shape
    line = n // 4
    chips = n // 2
    gx, gy = lax.axis_index("gx"), lax.axis_index("gy")
    pos, y, core = gx // 4, lax.rem(gx // 2, 2), lax.rem(gx, 2)
    chip = gx // 2
    rows_of = prior.shape[0] // m
    each = chosen.shape[2]
    tile = 256
    by_line, by_y = range(len(pieces) - 1), len(pieces) - 1

    def at(p, yy, c):
        return (p * 2 + yy) * 2 + c

    prior_in = pltpu.make_async_copy(prior_ref, prior, prior_sem)
    vec_in = pltpu.make_async_copy(vec_ref, held.at[gx], vec_sem)
    vec_in.start()
    prior_in.start()

    def old_copy(block):
        columns = pl.ds(pl.multiple_of(block * width, 128), width)
        return pltpu.make_async_copy(old_ref.at[:, columns], acc.at[:, columns], old_sem.at[block])

    barrier = pltpu.get_barrier_semaphore()
    for step in range(1, n):
        pl.semaphore_signal(barrier, inc=1, device_id=(lax.rem(gx + step, n), gy), device_id_type=MESH)
    for step in range(1, m):
        pl.semaphore_signal(barrier, inc=1, device_id=(gx, lax.rem(gy + step, m)), device_id_type=MESH)
    pl.semaphore_wait(barrier, n - 1 + m - 1)

    sent = []

    def send(copy, when=None):
        if when is None:
            copy.start()
        else:
            pl.when(when)(copy.start)
        sent.append((copy, when))

    def ways(p, yy, c):
        return at(p + 1, yy, c), at(p - 1, yy, c), at(p, 1 - yy, c), at(p, yy, 1 - c)

    targets = ways(pos, y, core)

    def piece_copy(src, piece, way):
        first_row, count = pieces[piece]
        part = held.at[src, pl.ds(first_row, count)]
        return pltpu.make_async_remote_copy(part, part, v_send.at[src, piece, way], v_recv.at[src, piece], device_id=(targets[way], gy), device_id_type=MESH)

    def arrived(src, piece):
        piece_copy(src, piece, 3).wait_recv()

    vec_in.wait()
    send(piece_copy(gx, by_y, 2))
    for piece in (*by_line, by_y):
        send(piece_copy(gx, piece, 0), pos + 1 < line)
        send(piece_copy(gx, piece, 1), pos > 0)
        if piece != by_y:
            send(piece_copy(gx, piece, 2))
    for step in range(1, m):
        copy = pltpu.make_async_remote_copy(held.at[gx], slab, s_send.at[step - 1], s_recv, device_id=(gx, lax.rem(gy + step, m)), device_id_type=MESH)
        send(copy, gy == 0)
    for piece in (*by_line, by_y):
        send(piece_copy(gx, piece, 3))

    prior_in.wait()
    for step in range(n):
        old_copy(step).start()
    keys = piv_ref.shape[1]
    local_index = jnp.broadcast_to(piv_ref[...], (keys, keys)).T[:, :1] - gx * prior.shape[0]
    onehot = (lax.broadcasted_iota(jnp.int32, (keys, prior.shape[0]), 1) == local_index).astype(F32).astype(BF16)

    def pick_tile(i, _):
        columns = pl.ds(pl.multiple_of(i * tile, tile), tile)
        wide[:, columns] = jnp.dot(onehot, prior[:, columns], preferred_element_type=F32)
        return 0
    lax.fori_loop(0, prior.shape[1] // tile, pick_tile, 0)
    for i in range(n):
        chosen[i // chips, i % chips] = wide[i * each:(i + 1) * each, :].astype(BF16)

    @pl.when(gy == 0)
    def _():
        own = pltpu.make_async_copy(vec_ref, slab, own_sem)
        own.start()
        own.wait()
    first = pltpu.make_async_remote_copy(chosen.at[1 - core], half_in, d_send.at[0], d_recv.at[0], device_id=(targets[3], gy), device_id_type=MESH)
    send(first)

    across = at(pos, 1 - y, core)
    arrived(across, by_y)
    send(piece_copy(across, by_y, 0), pos + 1 < line)
    send(piece_copy(across, by_y, 1), pos > 0)
    send(piece_copy(across, by_y, 3))

    first.wait_recv()
    for i in range(chips):
        half[i] = (chosen[core, i].astype(F32) + half_in[i].astype(F32)).astype(BF16)

    def sides(step):
        return ((0, pos - step, pos >= step), (1, pos + step, pos + step < line))

    def line_round(step, piece, yy, on_y):
        for way, src_pos, ok in sides(step):
            src = at(src_pos, yy, core)

            @pl.when(ok)
            def _():
                arrived(src, piece)
            onward = pos + 1 < line if way == 0 else pos > 0
            send(piece_copy(src, piece, way), jnp.logical_and(ok, onward))
            if on_y:
                send(piece_copy(src, piece, 2), ok)
            send(piece_copy(src, piece, 3), ok)

    def over_y(src_pos, ok):
        src = at(src_pos, 1 - y, core)
        for piece in by_line:
            if ok is None:
                arrived(src, piece)
            else:
                pl.when(ok)(functools.partial(arrived, src, piece))
            send(piece_copy(src, piece, 3), ok)

    def update(block):
        columns = pl.ds(pl.multiple_of(block * width, 128), width)

        def rows_step(i, _):
            rows = pl.ds(pl.multiple_of(i * tile, tile), tile)
            acc[rows, columns] += jnp.dot(slab_t[rows, :], held[block], preferred_element_type=F32)
            return 0
        lax.fori_loop(0, acc.shape[0] // tile, rows_step, 0)

    def updates(src_pos, yy, c, ok, wait):
        def go():
            src = at(src_pos, yy, c)
            if wait:
                for piece in range(len(pieces)):
                    arrived(src, piece)
            old_copy(src).wait()
            update(src)
        if ok is None:
            go()
        else:
            pl.when(ok)(go)

    for step in range(1, chips):
        other = lax.rem(chip + step, chips)
        send(pltpu.make_async_remote_copy(half.at[other], rs_in.at[step - 1], rs_send.at[step - 1], rs_recv.at[step - 1], device_id=(other * 2 + core, gy), device_id_type=MESH))

    for piece in by_line:
        line_round(1, piece, y, True)
    line_round(1, by_y, y, False)

    @pl.when(gy != 0)
    def _():
        pltpu.make_async_remote_copy(held.at[gx], slab, s_send.at[0], s_recv, device_id=(gx, gy), device_id_type=MESH).wait_recv()
    slab_t[...] = slab[...].T
    updates(pos, y, core, None, False)
    line_round(1, by_y, 1 - y, False)
    updates(pos, y, 1 - core, None, True)

    total = half[chip].astype(F32)
    for step in range(1, chips):
        pltpu.make_async_remote_copy(half.at[chip], rs_in.at[step - 1], rs_send.at[step - 1], rs_recv.at[step - 1], device_id=(gx, gy), device_id_type=MESH).wait_recv()
        total = total + rs_in[step - 1].astype(F32)
    pick[core, chip] = total.astype(BF16)

    over_y(pos, None)
    line_round(2, by_line[0], y, True)

    for step in range(1, chips):
        other = lax.rem(chip + step, chips)
        send(pltpu.make_async_remote_copy(pick.at[core, chip], pick.at[core, chip], ag_send.at[step - 1], ag_recv.at[step - 1], device_id=(other * 2 + core, gy), device_id_type=MESH))

    for way, src_pos, ok in sides(1):
        updates(src_pos, y, core, ok, False)
    for piece in by_line[1:]:
        line_round(2, piece, y, True)
    line_round(2, by_y, y, False)
    line_round(2, by_y, 1 - y, False)
    updates(pos, 1 - y, core, None, False)
    for way, src_pos, ok in sides(1):
        over_y(src_pos, ok)
        updates(src_pos, y, 1 - core, ok, True)

    for step in range(1, chips):
        other = lax.rem(chip + chips - step, chips)
        pltpu.make_async_remote_copy(pick.at[core, other], pick.at[core, other], ag_send.at[step - 1], ag_recv.at[step - 1], device_id=(gx, gy), device_id_type=MESH).wait_recv()
    last = pltpu.make_async_remote_copy(pick.at[core], pick.at[core], d_send.at[1], d_recv.at[1], device_id=(targets[3], gy), device_id_type=MESH)
    send(last)
    updates(pos, 1 - y, 1 - core, None, True)

    for step in range(3, line):
        for piece in by_line:
            line_round(step, piece, y, True)
        line_round(step, by_y, y, False)
        line_round(step, by_y, 1 - y, False)

    pltpu.make_async_remote_copy(pick.at[1 - core], pick.at[1 - core], d_send.at[1], d_recv.at[1], device_id=(gx, gy), device_id_type=MESH).wait_recv()
    for i in range(n):
        wide[i * each:(i + 1) * each, :] = pick[i // chips, i % chips].astype(F32)
    picked = wide[...].astype(BF16)

    def part_rows(g):
        def go(i, _):
            rows = pl.ds(pl.multiple_of(i * tile, tile), tile)
            source = pl.ds(pl.multiple_of(g * rows_of + i * tile, tile), tile)
            parts[g, rows, :] = lax.dot_general(prior[source, :], picked, (((1,), (1,)), ((), ())), preferred_element_type=F32).astype(BF16)
            return 0
        lax.fori_loop(0, rows_of // tile, go, 0)

    for g in range(m):
        part_rows(g)
    for way, src_pos, ok in sides(1):
        updates(src_pos, 1 - y, core, ok, False)
    for k in range(1, m):
        to = lax.rem(gy + k, m)
        send(pltpu.make_async_remote_copy(parts.at[to], parts_in.at[k - 1], p_send.at[k - 1], p_recv.at[k - 1], device_id=(gx, to), device_id_type=MESH))
    for way, src_pos, ok in sides(1):
        updates(src_pos, 1 - y, 1 - core, ok, True)

    for step in range(2, line):
        for way, src_pos, ok in sides(step):
            updates(src_pos, y, core, ok, False)
            over_y(src_pos, ok)
            updates(src_pos, y, 1 - core, ok, True)
        for way, src_pos, ok in sides(step):
            updates(src_pos, 1 - y, core, ok, False)
            if step < line - 1:
                updates(src_pos, 1 - y, 1 - core, ok, True)

    total = parts[gy].astype(F32)
    for k in range(1, m):
        pltpu.make_async_remote_copy(parts.at[gy], parts_in.at[k - 1], p_send.at[k - 1], p_recv.at[k - 1], device_id=(gx, gy), device_id_type=MESH).wait_recv()
        total = total + parts_in[k - 1].astype(F32)
    resid[...] = pair_ref[...] - total
    for way, src_pos, ok in sides(line - 1):
        updates(src_pos, 1 - y, 1 - core, ok, True)

    for copy, when in sent:
        if when is None:
            copy.wait_send()
        else:
            pl.when(when)(copy.wait_send)


def fused(n, m, old_block, vectors, prior, pair_columns, pivots):
    depth, width = vectors.shape[0], vectors.shape[2]
    rows, columns = old_block.shape
    keys, prior_width = pivots.shape[0], prior.shape[1]
    each, chips = keys // n, n // 2
    rows_of = prior.shape[0] // m
    unit = depth // 16
    pieces = ((0, 6 * unit), (6 * unit, 7 * unit), (13 * unit, depth - 13 * unit))
    dma = pltpu.SemaphoreType.DMA
    anywhere = pl.BlockSpec(memory_space=pl.ANY)
    vmem = pl.BlockSpec(memory_space=pltpu.VMEM)
    return pl.pallas_call(
        functools.partial(kernel, n, m, pieces),
        out_shape=(
            pltpu.VMEM((rows, columns), F32),
            jax.ShapeDtypeStruct(pair_columns.shape, F32),
        ),
        in_specs=[anywhere, anywhere, anywhere, vmem, vmem],
        out_specs=(vmem, vmem),
        scratch_shapes=[
            pltpu.VMEM((n, depth, width), BF16),
            pltpu.VMEM((width, depth), BF16),
            pltpu.VMEM((depth, width), BF16),
            pltpu.VMEM(prior.shape, BF16),
            pltpu.VMEM((keys, prior_width), F32),
            pltpu.VMEM((2, chips, each, prior_width), BF16),
            pltpu.VMEM((chips, each, prior_width), BF16),
            pltpu.VMEM((chips, each, prior_width), BF16),
            pltpu.VMEM((chips - 1, each, prior_width), BF16),
            pltpu.VMEM((2, chips, each, prior_width), BF16),
            pltpu.VMEM((m, rows_of, keys), BF16),
            pltpu.VMEM((m - 1, rows_of, keys), BF16),
            dma, dma, dma((n,)), dma,
            dma((n, 3, 4)), dma((n, 3)), dma((m - 1,)), dma, dma((2,)), dma((2,)),
            dma((chips - 1,)), dma((chips - 1,)), dma((chips - 1,)), dma((chips - 1,)), dma((m - 1,)), dma((m - 1,)),
        ],
        compiler_params=pltpu.CompilerParams(collective_id=0, has_side_effects=True, vmem_limit_bytes=25 * 1024 * 1024),
    )(vectors.reshape(depth, width), prior, old_block, pair_columns, pivots.reshape(1, keys))

def solution(mesh):
    n, m = mesh.shape["gx"], mesh.shape["gy"]

    def local(old_block, vectors, prior, pair_columns, pivots):
        width = vectors.shape[2]
        whole_tiles = width % 256 == 0 and prior.shape[1] % 256 == 0 and prior.shape[0] // m % 256 == 0
        if n % 4 == 0 and n >= 12 and m >= 2 and pivots.shape[0] % (8 * n) == 0 and whole_tiles:
            return fused(n, m, old_block, vectors, prior, pair_columns, pivots)
        return plain(old_block, vectors, prior, pair_columns, pivots)

    placed = (P("gx", "gy"), P(None, "gy", "gx"), P("gx", "gy"), P(("gx", "gy"), None), P())
    return jax.shard_map(
        local,
        mesh=mesh,
        in_specs=placed,
        out_specs=(P("gx", "gy"), P(("gx", "gy"), None)),
        check_vma=False,
    )
```

time: 78.1 us -> 78.2 us (level)
  Pallas kernels: 61.6 us -> 63.5 us
  local copies, waits for them, and re-layouts: 15.3 us -> 13.9 us
    pallas_call x1, Pallas kernels: 61.6 us -> 63.5 us  [fused(): pl.pallas_call(functools.partial(kernel, n, m, pieces), out_shape=(pltpu....]
    reshape x1 -> x0, local copies, waits for them, and re-layouts: 1.39 us -> none  [fused(): pivots.reshape(keys, 1)]
where the time goes in v2:
time: 78.2 us; the launch traced here: 78 us
  Pallas kernels  63.5 us (81%)
  local copies, waits for them, and re-layouts  13.9 us (18%)
    pallas_call x1, Pallas kernels, fused(): pl.pallas_call(functools.partial(kernel, n, m, pieces), out_shape=(pltpu....  63.5 us
    unnamed x4, local copies, waits for them, and re-layouts  13.9 us

profile of v2, /device:TPU:0, one launch (start us, length us, event | category | flops | bytes accessed | tf_op | source)
XLA Modules:
  0.0 78.0 jit_solution(3866384763154356274)
XLA Ops:
  0.6 63.5 %shard_map.68 = (f32[768,12288]{1,0:T(8,128)S(1)}, f32[1024,128]{1,0:T(8,128)}) custom-call(bf16[256,768]{1,0:T(8,128)(2,1)} %bitcast.2, bf16[2048,1536]{1,0:T(8,128)(2,1)} %prior_ref.1, f32[768,12288]{1,0:T(8,128)} %old_ref.1, f32[1024,128]{1,0:T(8,128)} %pair_ref.1, s32[1,128]{1,0:T(1,128)} %bitcast.3), custom_call_target="tpu_custom_call" | custom-call | tf_op jit(solution)/shard_map/pallas_call | solution.py:297
  64.2 0.0 copy-start
  64.2 13.1 %copy.9 = f32[768,12288]{1,0:T(8,128)} copy(f32[768,12288]{1,0:T(8,128)S(1)} %get-tuple-element.2) | data formatting | bytes 75497472
  77.2 0.0 copy-done
  77.2 0.8 %copy.10 = f32[1024,128]{1,0:T(8,128)} copy(f32[1024,128]{1,0:T(8,128)S(1)} %copy-done) | data formatting | bytes 1048576
Async XLA Ops:
  64.2 13.1 %copy-start = (f32[1024,128]{1,0:T(8,128)S(1)}, f32[1024,128]{1,0:T(8,128)}, u32[]{:S(2)}) copy-start(f32[1024,128]{1,0:T(8,128)} %get-tuple-element.7) | copy-start | bytes 1572868
